TPU v7x, 32 devices: a whole 2x2x4 slice. The times are simulated.
32 devices in a mesh: alpha: 8 (over y, x, core), beta: 4 (over z).
Axes of the slice: x: 2, y: 2, z: 4, core: 2. Of those that a mesh axis runs over, the one named last changes fastest.
Arguments:
- ci_vector: bfloat16 [1024, 2048], P('alpha', 'beta'), may hold values from -6 to 6
- alpha_tiles: bfloat16 [8, 8, 4, 128, 128], P(None, 'alpha'), may hold values from -0.25 to 0.25
- alpha_list: int32 [8, 8, 4], P(None, 'alpha'), may hold values from 0 to 7, as said below
- alpha_count: int32 [8, 8], P(None, 'alpha'), may hold values from 1 to 4, as said below
- beta_tiles: bfloat16 [8, 16, 4, 128, 128], P(None, 'beta'), may hold values from -0.09375 to 0.09375
- beta_target: int32 [8, 16, 4], P(None, 'beta'), may hold values from 0 to 15
- alpha_diag: float32 [1024], P('alpha'), may hold values from -6 to 6
- beta_diag: float32 [2048], P('beta'), may hold values from -6 to 6
Outputs:
- sigma_vector: float32 [1024, 2048], P('alpha', 'beta')
Inputs may be any that keep to these rules, and one draw needn't show every extreme that they name: `alpha_list`: the 4 entries of one factor and block are distinct alpha blocks within 3 blocks of that block. `alpha_count`: some alpha block has 4 live slots in every factor.
All inputs are finite; a program needn't handle non-finite values.
Results may differ from a plain program's by a relative error of at most 0.007.
Values may be sent and summed in bfloat16 or wider, within the bound.
No kernel may reach another device: no remote copies, remote signals or barrier semaphores. Data moves between devices by JAX's collectives and lax.ppermute only.
A program may use at most 64 MiB of HBM per device.

v0:
```python
import jax
import jax.numpy as jnp
from jax import lax
from jax.sharding import PartitionSpec as P

BAND = 3


def from_behind(shard, axis, by):
    length = lax.axis_size(axis)
    return lax.ppermute(shard, axis, [(i, (i + by) % length) for i in range(length)])


def shards(
    ci_vector, alpha_tiles, alpha_list, alpha_count, beta_tiles, beta_target, alpha_diag, beta_diag
):
    tile_size = ci_vector.shape[0]
    factors = alpha_tiles.shape[0]
    local_blocks = beta_tiles.shape[1]
    slot_count = beta_tiles.shape[2]
    target_count = local_blocks * lax.axis_size("beta")
    own_block = lax.axis_index("alpha")
    window = ci_vector[None]
    covered = 0
    while covered < BAND:
        widened = min(3 * covered + 1, BAND)
        needed = widened - covered
        distance = 2 * covered + 1
        below_part = from_behind(window[distance - needed :], "alpha", distance)
        above_part = from_behind(window[:needed], "alpha", -distance)
        window = jnp.concatenate([below_part, window, above_part], axis=0)
        covered = widened
    positions = alpha_list[:, 0, :] - own_block + BAND
    counts = alpha_count[:, 0]
    own_tiles = alpha_tiles[:, 0]
    slot_mask = jnp.arange(own_tiles.shape[1], dtype=jnp.int32)[None, :] < counts[:, None]
    masked = jnp.where(slot_mask[..., None, None], own_tiles, jnp.zeros((), own_tiles.dtype))
    picked = window[positions]
    coupled = jnp.einsum(
        "fksr,fkrc->fsc", masked, picked, preferred_element_type=jnp.float32
    ).astype(jnp.bfloat16)
    source = coupled.reshape(factors, tile_size, local_blocks, tile_size)
    contrib = jnp.einsum(
        "frsi,fskij->fskrj", source, beta_tiles, preferred_element_type=jnp.float32
    )
    contrib = contrib.reshape(factors * local_blocks * slot_count, tile_size, tile_size)
    by_target = jax.ops.segment_sum(contrib, beta_target.reshape(-1), num_segments=target_count)
    partial_value = by_target.transpose(1, 0, 2).reshape(tile_size, target_count * tile_size)
    summed = lax.psum_scatter(
        partial_value.astype(jnp.bfloat16), "beta", scatter_dimension=1, tiled=True
    ).astype(jnp.float32)
    return summed + (alpha_diag[:, None] + beta_diag[None, :]) * ci_vector.astype(jnp.float32)


def solution(mesh):
    placed = (
        P("alpha", "beta"),
        P(None, "alpha", None, None, None),
        P(None, "alpha", None),
        P(None, "alpha"),
        P(None, "beta", None, None, None),
        P(None, "beta", None),
        P("alpha"),
        P("beta"),
    )
    return jax.shard_map(
        shards, mesh=mesh, in_specs=placed, out_specs=P("alpha", "beta"), check_vma=False
    )
```

profile of v0, /device:TPU:0, one launch (start us, length us, event | category | flops | bytes accessed | tf_op | source)
XLA Modules:
  0.0 89.4 jit_solution(10544557474676056248)
XLA Ops:
  6.5 0.0 reduce-scatter.2.cloned.1.call-start
  6.5 3.4 %collective-permute-start = (bf16[1,128,512]{2,1,0:T(8,128)(2,1)}, bf16[1,128,512]{2,1,0:T(8,128)(2,1)S(1)}, u32[]{:S(2)}, u32[]{:S(2)}) collective-permute-start(bf16[1,128,512]{2,1,0:T(8,128)(2,1)} %bitcast.29), channel_id=1, source_target_pairs={{0,28},{4,0},{8,4},{12,8},{16,12},{20,16},{24,20},{28,24},{1,29},{... | collective-permute-start | bytes 393224 | tf_op jit(solution)/shard_map/ppermute | solution.py:11
  9.9 0.0 collective-permute-start.2
  9.9 0.7 compare_select_fusion
  10.6 0.1 copy.16
  10.7 0.1 reshape.64
  10.8 2.4 %collective-permute-done = bf16[1,128,512]{2,1,0:T(8,128)(2,1)S(1)} collective-permute-done((bf16[1,128,512]{2,1,0:T(8,128)(2,1)}, bf16[1,128,512]{2,1,0:T(8,128)(2,1)S(1)}, u32[]{:S(2)}, u32[]{:S(2)}) %collective-permute-start) | collective-permute-done | bytes 131104 | tf_op jit(solution)/shard_map/ppermute | solution.py:11
  13.1 2.3 %collective-permute-done.2 = bf16[1,128,512]{2,1,0:T(8,128)(2,1)S(1)} collective-permute-done((bf16[1,128,512]{2,1,0:T(8,128)(2,1)}, bf16[1,128,512]{2,1,0:T(8,128)(2,1)S(1)}, u32[]{:S(2)}, u32[]{:S(2)}) %collective-permute-start.2) | collective-permute-done | bytes 131104 | tf_op jit(solution)/shard_map/ppermute | solution.py:11
  15.4 1.0 %pad_maximum_fusion.1 = (bf16[2,128,512]{2,1,0:T(8,128)(2,1)S(1)}, bf16[2,128,512]{2,1,0:T(8,128)(2,1)S(1)}) fusion(bf16[1,128,512]{2,1,0:T(8,128)(2,1)} %bitcast.31, bf16[1,128,512]{2,1,0:T(8,128)(2,1)S(1)} %collective-permute-done.2, bf16[1,128,512]{2,1,0:T(8,128)(2,1)S(1)} %collective-permute-done), kind=kLoop, calls=%fused_computation.10 | loop fusion | flops 262144 | bytes 917504 | tf_op jit(solution)/shard_map/concatenate | solution.py:31
  16.4 0.5 collective-permute-start.1
  16.9 0.8 copy.15
  17.7 0.1 reshape.72
  17.8 0.7 iota_compare_fusion
  18.5 1.3 %collective-permute-start.3 = (bf16[2,128,512]{2,1,0:T(8,128)(2,1)S(1)}, bf16[2,128,512]{2,1,0:T(8,128)(2,1)S(1)}, u32[]{:S(2)}, u32[]{:S(2)}) collective-permute-start(bf16[2,128,512]{2,1,0:T(8,128)(2,1)S(1)} %get-tuple-element.5), channel_id=1, source_target_pairs={{0,20},{4,24},{8,28},{12,0},{16,4},{20,8},{24,12},{28,16},{1,21},{... | collective-permute-start | bytes 786440 | tf_op jit(solution)/shard_map/ppermute | solution.py:11
  19.9 7.4 %collective-permute-done.1 = bf16[2,128,512]{2,1,0:T(8,128)(2,1)S(1)} collective-permute-done((bf16[2,128,512]{2,1,0:T(8,128)(2,1)S(1)}, bf16[2,128,512]{2,1,0:T(8,128)(2,1)S(1)}, u32[]{:S(2)}, u32[]{:S(2)}) %collective-permute-start.1) | collective-permute-done | bytes 262176 | tf_op jit(solution)/shard_map/ppermute | solution.py:11
  27.3 0.9 %constant_dynamic-update-slice_fusion.2 = bf16[7,128,512]{2,1,0:T(8,128)(2,1)S(1)} fusion(bf16[7,128,512]{2,1,0:T(8,128)(2,1)S(1)} %constant_dynamic-update-slice_fusion.3, bf16[128,512]{1,0:T(8,128)(2,1)} %param.8), kind=kLoop, calls=%fused_computation.14 | loop fusion | bytes 262144
  28.2 0.0 collective-permute-done.3
  28.3 0.0 copy-start
  28.3 2.8 %gather_fusion = bf16[32,128,512]{2,1,0:T(8,128)(2,1)} fusion(bf16[7,128,512]{2,1,0:T(8,128)(2,1)S(1)} %constant_dynamic-update-slice_fusion, s32[1024]{0:T(1024)S(1)} %pad_clamp_fusion), kind=kCustom, calls=%fused_computation | custom fusion | bytes 8388736 | tf_op jit(solution)/shard_map/gather | solution.py:38
  31.0 0.0 copy-done
  31.0 2.9 %bitcast_convert_fusion = bf16[8,128,512]{2,1,0:T(8,128)(2,1)S(1)} fusion(bf16[8,4,128,512]{3,2,1,0:T(8,128)(2,1)} %bitcast.26, bf16[8,1,4,128,128]{4,3,2,1,0:T(8,128)(2,1)S(1)} %copy-done, pred[8,4]{1,0:T(8,128)(4,1)S(1)} %iota_compare_fusion), kind=kOutput, calls=%fused_computation.2 | convolution fusion | flops 537919488 | bytes 6291488 | tf_op jit(solution)/shard_map/fksr,fkrc->fsc/dot_general | solution.py:39
  34.0 0.3 reshape.60
  34.3 6.7 %fusion = f32[8,4,128,4,128]{4,2,3,1,0:T(8,128)} fusion(bf16[8,4,4,128,128]{4,3,2,1,0:T(8,128)(2,1)} %param.12, bf16[8,128,4,128,1]{3,2,1,0,4:T(4,128)(2,1)S(1)} %bitcast.27), kind=kOutput, calls=%fused_computation.3 | convolution fusion | flops 536870912 | bytes 13631488 | tf_op jit(solution)/shard_map/frsi,fskij->fskrj/dot_general | solution.py:43
  40.9 0.1 broadcast_in_dim.23
  41.0 0.0 copy-start.1
  41.1 0.0 copy-start.2
  41.1 0.0 copy-start.3
  41.1 17.0 %scatter_fusion = f32[16,128,128]{2,1,0:T(8,128)S(1)} fusion(f32[16,128,128]{2,1,0:T(8,128)S(1)} %broadcast_in_dim.23, s32[128]{0:T(128)S(1)} %reshape.72, f32[128,128,128]{2,1,0:T(8,128)} %bitcast.25), kind=kCustom, calls=%fused_computation.1 | custom fusion | flops 2097152 | bytes 25166336 | tf_op jit(solution)/shard_map/scatter-add | solution.py:47
  58.1 0.1 convert_bitcast_fusion
  58.2 1.0 %copy.18 = bf16[128,16,128]{0,2,1:T(8,128)(2,1)} copy(bf16[128,16,128]{2,0,1:T(8,128)(2,1)S(1)} %convert_bitcast_fusion) | data formatting | bytes 1048576 | tf_op jit(solution)/shard_map/convert_element_type | solution.py:50
  59.2 0.0 reduce-scatter.2.cloned.1.call-update
  59.3 0.0 copy-done.1
  59.3 0.1 copy.19
  59.4 21.2 %reduce-scatter.2.cloned.1.call-done = bf16[128,512]{0,1:T(8,128)(2,1)} async-done(((bf16[128,2048]{0,1:T(8,128)(2,1)}), bf16[128,512]{0,1:T(8,128)(2,1)}) %reduce-scatter.2.cloned.1.call-update) | async-done | bytes 131088 | tf_op jit(solution)/shard_map/reduce_scatter | solution.py:49
  80.6 0.0 copy-done.2
  80.6 0.0 copy-done.3
  80.6 1.0 %multiply_add_fusion = f32[128,512]{0,1:T(8,128)S(1)} fusion(bf16[128,512]{0,1:T(8,128)(2,1)S(1)} %copy.19, bf16[128,512]{0,1:T(8,128)(2,1)} %reduce-scatter.2.cloned.1.call-done, f32[512]{0:T(512)S(1)} %copy-done.2, f32[128]{0:T(128)S(1)} %copy-done.3), kind=kLoop, calls=%fused_computation.11 | loop fusion | flops 327680 | bytes 526848 | tf_op jit(solution)/shard_map/add | solution.py:52
  81.7 0.8 copy.20
  (5 shorter events, 0.1 us)
Async XLA Ops:
  6.5 74.1 %reduce-scatter.2.cloned.1.call-start = ((), (), s32[]{:S(2)}) async-start(), calls=%async_computation.1 | async-start | bytes 655360 | tf_op jit(solution)/shard_map/reduce_scatter | solution.py:49
  6.5 6.6 %collective-permute-start = (bf16[1,128,512]{2,1,0:T(8,128)(2,1)}, bf16[1,128,512]{2,1,0:T(8,128)(2,1)S(1)}, u32[]{:S(2)}, u32[]{:S(2)}) collective-permute-start(bf16[1,128,512]{2,1,0:T(8,128)(2,1)} %bitcast.29), channel_id=1, source_target_pairs={{0,28},{4,0},{8,4},{12,8},{16,12},{20,16},{24,20},{28,24},{1,29},{... | collective-permute-start | bytes 393224 | tf_op jit(solution)/shard_map/ppermute | solution.py:11
  9.9 5.5 %collective-permute-start.2 = (bf16[1,128,512]{2,1,0:T(8,128)(2,1)}, bf16[1,128,512]{2,1,0:T(8,128)(2,1)S(1)}, u32[]{:S(2)}, u32[]{:S(2)}) collective-permute-start(bf16[1,128,512]{2,1,0:T(8,128)(2,1)} %bitcast.30), channel_id=1, source_target_pairs={{0,4},{4,8},{8,12},{12,16},{16,20},{20,24},{24,28},{28,0},{1,5},{5... | collective-permute-start | bytes 393224 | tf_op jit(solution)/shard_map/ppermute | solution.py:11
  16.4 10.8 %collective-permute-start.1 = (bf16[2,128,512]{2,1,0:T(8,128)(2,1)S(1)}, bf16[2,128,512]{2,1,0:T(8,128)(2,1)S(1)}, u32[]{:S(2)}, u32[]{:S(2)}) collective-permute-start(bf16[2,128,512]{2,1,0:T(8,128)(2,1)S(1)} %get-tuple-element.6), channel_id=1, source_target_pairs={{0,12},{4,16},{8,20},{12,24},{16,28},{20,0},{24,4},{28,8},{1,13},{... | collective-permute-start | bytes 786440 | tf_op jit(solution)/shard_map/ppermute | solution.py:11
  18.5 9.7 %collective-permute-start.3 = (bf16[2,128,512]{2,1,0:T(8,128)(2,1)S(1)}, bf16[2,128,512]{2,1,0:T(8,128)(2,1)S(1)}, u32[]{:S(2)}, u32[]{:S(2)}) collective-permute-start(bf16[2,128,512]{2,1,0:T(8,128)(2,1)S(1)} %get-tuple-element.5), channel_id=1, source_target_pairs={{0,20},{4,24},{8,28},{12,0},{16,4},{20,8},{24,12},{28,16},{1,21},{... | collective-permute-start | bytes 786440 | tf_op jit(solution)/shard_map/ppermute | solution.py:11
  28.3 2.8 %copy-start = (bf16[8,1,4,128,128]{4,3,2,1,0:T(8,128)(2,1)S(1)}, bf16[8,1,4,128,128]{4,3,2,1,0:T(8,128)(2,1)}, u32[]{:S(2)}) copy-start(bf16[8,1,4,128,128]{4,3,2,1,0:T(8,128)(2,1)} %param.9) | copy-start | bytes 3145732
  41.0 18.2 %copy-start.1 = (bf16[128,512]{1,0:T(8,128)(2,1)S(1)}, bf16[128,512]{1,0:T(8,128)(2,1)}, u32[]{:S(2)}) copy-start(bf16[128,512]{1,0:T(8,128)(2,1)} %param.8) | copy-start | bytes 393220
  41.1 39.6 %copy-start.2 = (f32[512]{0:T(512)S(1)}, f32[512]{0:T(512)}, u32[]{:S(2)}) copy-start(f32[512]{0:T(512)} %param.15) | copy-start | bytes 6148
  41.1 39.6 %copy-start.3 = (f32[128]{0:T(128)S(1)}, f32[128]{0:T(128)}, u32[]{:S(2)}) copy-start(f32[128]{0:T(128)} %param.14) | copy-start | bytes 1540
Sparse Core Ops, SparseCore 0:
  59.4 21.1 reduce-scatter.1
where the time goes:
time: 90 us; the launch traced here: 89.4 us
  waiting for transfers between devices  33.3 us (37%)
  other arithmetic  20.6 us (23%)
  between operations  13.5 us (15%)
  matrix products  9.6 us (11%)
  local copies, waits for them, and re-layouts  7.18 us (8%)
  starting transfers between devices  5.16 us (6%)
    reduce_scatter x1, waiting for transfers between devices, shards(): lax.psum_scatter(partial_value.astype(jnp.bfloat16), 'beta', scatter_dime...  21.2 us
    scatter-add x1, other arithmetic, shards(): jax.ops.segment_sum(contrib, beta_target.reshape(-1), num_segments=target...  17 us
    ppermute x4, waiting for transfers between devices, from_behind(): lax.ppermute(shard, axis, [(i, (i + by) % length) for i in range(length)])  12 us
    dot_general x1, matrix products, shards(): jnp.einsum('frsi,fskij->fskrj', source, beta_tiles, preferred_element_typ...  6.65 us
    ppermute x4, starting transfers between devices, from_behind(): lax.ppermute(shard, axis, [(i, (i + by) % length) for i in range(length)])  5.16 us
    dot_general x1, matrix products, shards(): jnp.einsum('fksr,fkrc->fsc', masked, picked, preferred_element_type=jnp.f...  2.94 us
    gather x1, local copies, waits for them, and re-layouts, shards(): picked = window[positions]  2.76 us
    unnamed x14, local copies, waits for them, and re-layouts  1.89 us
  transfers between devices with their start and end apart: 5, of which 4 were waited for; matrix products, arithmetic and copies ran while one was open for 4% of the time, Pallas kernels for 0%

commit v1 on v0

v1 whole, which is shorter than its diff:
```python
import jax
import jax.numpy as jnp
from jax import lax
from jax.experimental import pallas as pl
from jax.experimental.pallas import tpu as pltpu
from jax.sharding import PartitionSpec as P

BAND = 3


def exchange(shard, axis, pairs):
    return lax.ppermute(shard, axis, pairs)


def band_window(ci_vector):
    length = lax.axis_size("alpha")
    pieces = []
    for offset in range(-BAND, BAND + 1):
        if offset == 0:
            pieces.append(ci_vector)
        else:
            pairs = [(i, i - offset) for i in range(length) if 0 <= i - offset < length]
            pieces.append(exchange(ci_vector, "alpha", pairs))
    return dict(enumerate(pieces)), lambda block, own: block - own + BAND


def cube_window(ci_vector):
    length = lax.axis_size("alpha")

    def wanted(i, source):
        return abs(i - source) <= BAND

    pieces = [None] * length
    pieces[0] = ci_vector
    plans = {}
    for k in range(2, length, 2):
        odd = [(i ^ (k + 1), i) for i in range(length) if wanted(i, i ^ (k + 1))]
        even = [(i ^ k, i) for i in range(length) if wanted(i, i ^ k)]
        plans[k] = (even, odd)
    swap = [(i, i ^ 1) for i in range(length)]
    for k, (even, odd) in sorted(plans.items(), reverse=True):
        if not even:
            if odd:
                pieces[k + 1] = exchange(ci_vector, "alpha", odd)
            continue
        relayed = [(i ^ k, i) for i in range(length) if wanted(i, i ^ k) or wanted(i ^ 1, i ^ k)]
        pieces[k] = exchange(ci_vector, "alpha", relayed)
    pieces[1] = exchange(ci_vector, "alpha", swap)
    for k, (even, odd) in sorted(plans.items()):
        if even and odd:
            pairs = [(i ^ 1, i) for _, i in odd]
            pieces[k + 1] = exchange(pieces[k], "alpha", pairs)
    held = {k: piece for k, piece in enumerate(pieces) if piece is not None}
    return held, lambda block, own: block ^ own


def term_kernel(
    sizes, place_of, sources, counts, targets, pieces, alpha_tiles, beta_tiles, outs, window, total
):
    factors, alpha_slots, local_blocks, beta_slots, groups, by_xor = sizes
    tile_size = total.shape[1]
    own_block, own_group = lax.axis_index("alpha"), lax.axis_index("beta")
    for place, piece in pieces.items():
        window[place] = piece[...]
    for block in range(total.shape[0]):
        total[block] = jnp.zeros(total.shape[1:], jnp.float32)
    for factor in range(factors):
        left, right = [], []
        for slot in range(alpha_slots):
            tile = alpha_tiles[factor, 0, slot]
            left.append(jnp.where(slot < counts[factor, 0], tile, jnp.zeros_like(tile)))
            right.append(window[place_of(sources[factor, 0, slot], own_block)])
        coupled = jnp.dot(
            jnp.concatenate(left, axis=1),
            jnp.concatenate(right, axis=0),
            preferred_element_type=jnp.float32,
        ).astype(jnp.bfloat16)
        for block in range(local_blocks):
            source = coupled[:, block * tile_size : (block + 1) * tile_size]
            tiles = [beta_tiles[factor, block, slot] for slot in range(beta_slots)]
            added = jnp.dot(source, jnp.concatenate(tiles, axis=1), preferred_element_type=jnp.float32)
            for slot in range(beta_slots):
                target = targets[factor, block, slot]
                group = target // local_blocks
                away = (group ^ own_group) if by_xor else lax.rem(group - own_group + groups, groups)
                place = away * local_blocks + lax.rem(target, local_blocks)
                total[place] += added[:, slot * tile_size : (slot + 1) * tile_size]
    for away in range(groups):
        for block in range(local_blocks):
            value = total[away * local_blocks + block].astype(jnp.bfloat16)
            outs[away][:, block * tile_size : (block + 1) * tile_size] = value


def shards(
    ci_vector, alpha_tiles, alpha_list, alpha_count, beta_tiles, beta_target, alpha_diag, beta_diag
):
    tile_size, columns = ci_vector.shape
    factors, _, alpha_slots = alpha_list.shape
    _, local_blocks, beta_slots = beta_target.shape
    length, groups = lax.axis_size("alpha"), lax.axis_size("beta")
    small = length & (length - 1) == 0 and length <= 2 * (BAND + 1)
    pieces, place_of = cube_window(ci_vector) if small else band_window(ci_vector)
    by_xor = groups & (groups - 1) == 0
    sizes = (factors, alpha_slots, local_blocks, beta_slots, groups, by_xor)

    def body(sources, counts, targets, *refs):
        n = len(pieces)
        held = dict(zip(pieces, refs[:n]))
        a_ref, b_ref, *outs = refs[n:-2]
        term_kernel(sizes, place_of, sources, counts, targets, held, a_ref, b_ref, outs, *refs[-2:])

    vmem = pl.BlockSpec(memory_space=pltpu.VMEM)
    smem = pl.BlockSpec(memory_space=pltpu.SMEM)
    flops = 2 * factors * tile_size * columns * tile_size * (alpha_slots + beta_slots)
    own, *far = pl.pallas_call(
        body,
        out_shape=[jax.ShapeDtypeStruct((tile_size, columns), jnp.bfloat16)] * groups,
        in_specs=[smem] * 3 + [vmem] * (len(pieces) + 2),
        out_specs=[vmem] * groups,
        scratch_shapes=[
            pltpu.VMEM((max(pieces) + 1, tile_size, columns), jnp.bfloat16),
            pltpu.VMEM((groups * local_blocks, tile_size, tile_size), jnp.float32),
        ],
        compiler_params=pltpu.CompilerParams(vmem_limit_bytes=20 * 2**20),
        cost_estimate=pl.CostEstimate(
            flops=flops, bytes_accessed=alpha_tiles.size * 2 + beta_tiles.size * 2, transcendentals=0
        ),
        name="couple",
    )(alpha_list, alpha_count, beta_target, *pieces.values(), alpha_tiles, beta_tiles)
    summed = own.astype(jnp.float32)
    received = {}
    for away in sorted(range(1, groups), key=lambda d: (d == 1, d)):
        if by_xor:
            pairs = [(i, i ^ away) for i in range(groups)]
        else:
            pairs = [(i, (i + away) % groups) for i in range(groups)]
        received[away] = exchange(far[away - 1], "beta", pairs)
    for away in sorted(received):
        summed = summed + received[away].astype(jnp.float32)
    return summed + (alpha_diag[:, None] + beta_diag[None, :]) * ci_vector.astype(jnp.float32)


def solution(mesh):
    placed = (
        P("alpha", "beta"),
        P(None, "alpha", None, None, None),
        P(None, "alpha", None),
        P(None, "alpha"),
        P(None, "beta", None, None, None),
        P(None, "beta", None),
        P("alpha"),
        P("beta"),
    )
    return jax.shard_map(
        shards, mesh=mesh, in_specs=placed, out_specs=P("alpha", "beta"), check_vma=False
    )
```

time: 90 us -> 38.9 us (0.43)
  waiting for transfers between devices: 33.3 us -> 13.5 us
  other arithmetic: 20.6 us -> 0.81 us
  between operations: 13.5 us -> 0.07 us
  matrix products: 9.6 us -> 0 us
  starting transfers between devices: 5.16 us -> 13.7 us
  Pallas kernels: 0 us -> 3.83 us
    reduce_scatter x1 -> x0, waiting for transfers between devices: 21.2 us -> none  [shards(): lax.psum_scatter(partial_value.astype(jnp.bfloat16), 'beta', scatter_dime...]
    scatter-add x1 -> x0, other arithmetic: 17 us -> none  [shards(): jax.ops.segment_sum(contrib, beta_target.reshape(-1), num_segments=target...]
    dot_general x2 -> x0, matrix products: 9.6 us -> none  [the longest x1 6.65 us: shards(): jnp.einsum('frsi,fskij->fskrj', source, beta_tiles, preferred_element_typ...]
    ppermute x4 -> x9, starting transfers between devices: 5.16 us -> 13.7 us  [exchange(): return lax.ppermute(shard, axis, pairs)]
    unnamed x14 -> x13, local copies, waits for them, and re-layouts: 1.89 us -> 6.6 us
    pallas_call x0 -> x1, Pallas kernels: none -> 3.83 us  [shards(): pl.pallas_call(body, out_shape=[jax.ShapeDtypeStruct((tile_size, columns)...]
    gather x1 -> x0, local copies, waits for them, and re-layouts: 2.76 us -> none  [shards(): picked = window[positions]]
    ppermute x4 -> x9, waiting for transfers between devices: 12 us -> 13.5 us  [exchange(): return lax.ppermute(shard, axis, pairs)]
  transfers between devices with their start and end apart: 5 -> 9, of which waited for: 4 -> 3; matrix products, arithmetic and copies ran while one was open for 4% -> 6% of each run, Pallas kernels for 0% -> 0%
where the time goes in v1:
time: 38.9 us; the launch traced here: 38.6 us
  starting transfers between devices  13.7 us (35%)
  waiting for transfers between devices  13.5 us (35%)
  local copies, waits for them, and re-layouts  6.6 us (17%)
  Pallas kernels  3.83 us (10%)
  other arithmetic  0.81 us (2%)
    ppermute x9, starting transfers between devices, exchange(): return lax.ppermute(shard, axis, pairs)  13.7 us
    ppermute x9, waiting for transfers between devices, exchange(): return lax.ppermute(shard, axis, pairs)  13.5 us
    unnamed x13, local copies, waits for them, and re-layouts  6.6 us
    pallas_call x1, Pallas kernels, shards(): pl.pallas_call(body, out_shape=[jax.ShapeDtypeStruct((tile_size, columns)...  3.83 us
    add x1, other arithmetic, shards(): summed + (alpha_diag[:, None] + beta_diag[None, :]) * ci_vector.astype(jn...  0.81 us
  transfers between devices with their start and end apart: 9, of which 3 were waited for; matrix products, arithmetic and copies ran while one was open for 6% of the time, Pallas kernels for 0%

profile of v1, /device:TPU:0, one launch (start us, length us, event | category | flops | bytes accessed | tf_op | source)
XLA Modules:
  0.0 38.6 jit_solution(10584935536929296978)
XLA Ops:
  0.0 0.0 copy-start.3
  0.0 0.0 copy-start.4
  0.0 0.8 %collective-permute-start.4 = (bf16[128,512]{1,0:T(8,128)(2,1)}, bf16[128,512]{1,0:T(8,128)(2,1)S(1)}, u32[]{:S(2)}, u32[]{:S(2)}) collective-permute-start(bf16[128,512]{1,0:T(8,128)(2,1)} %refs_0_.1), channel_id=1, source_target_pairs={{16,8},{20,12},{8,16},{12,20},{17,9},{21,13},{9,17},{13,21},{18,10... | collective-permute-start | bytes 393224 | tf_op jit(solution)/shard_map/ppermute | solution.py:12
  0.8 5.8 %collective-permute-start.1 = (bf16[128,512]{1,0:T(8,128)(2,1)}, bf16[128,512]{1,0:T(8,128)(2,1)S(1)}, u32[]{:S(2)}, u32[]{:S(2)}) collective-permute-start(bf16[128,512]{1,0:T(8,128)(2,1)} %refs_0_.1), channel_id=1, source_target_pairs={{8,0},{12,4},{0,8},{4,12},{24,16},{28,20},{16,24},{20,28},{9,1},{1... | collective-permute-start | bytes 393224 | tf_op jit(solution)/shard_map/ppermute | solution.py:12
  6.6 0.7 %collective-permute-start.3 = (bf16[128,512]{1,0:T(8,128)(2,1)}, bf16[128,512]{1,0:T(8,128)(2,1)S(1)}, u32[]{:S(2)}, u32[]{:S(2)}) collective-permute-start(bf16[128,512]{1,0:T(8,128)(2,1)} %refs_0_.1), channel_id=1, source_target_pairs={{16,4},{24,12},{4,16},{12,24},{17,5},{25,13},{5,17},{13,25},{18,6}... | collective-permute-start | bytes 393224 | tf_op jit(solution)/shard_map/ppermute | solution.py:12
  7.2 1.4 %collective-permute-start = (bf16[128,512]{1,0:T(8,128)(2,1)}, bf16[128,512]{1,0:T(8,128)(2,1)S(1)}, u32[]{:S(2)}, u32[]{:S(2)}) collective-permute-start(bf16[128,512]{1,0:T(8,128)(2,1)} %refs_0_.1), channel_id=1, source_target_pairs={{0,4},{4,0},{8,12},{12,8},{16,20},{20,16},{24,28},{28,24},{1,5},{5... | collective-permute-start | bytes 393224 | tf_op jit(solution)/shard_map/ppermute | solution.py:12
  8.7 0.0 collective-permute-done.4.refs_5_
  8.7 0.7 %collective-permute-start.5 = (bf16[128,512]{1,0:T(8,128)(2,1)S(1)}, bf16[128,512]{1,0:T(8,128)(2,1)S(1)}, u32[]{:S(2)}, u32[]{:S(2)}) collective-permute-start(bf16[128,512]{1,0:T(8,128)(2,1)S(1)} %collective-permute-done.4.refs_5_), channel_id=1, source_target_pairs={{12,8},{8,12},{20,16},{16,20},{13,9},{9,13},{21,17},{17,21},{14,10... | collective-permute-start | bytes 393224 | tf_op jit(solution)/shard_map/ppermute | solution.py:12
  9.3 3.4 %collective-permute-done.1.refs_2_ = bf16[128,512]{1,0:T(8,128)(2,1)S(1)} collective-permute-done((bf16[128,512]{1,0:T(8,128)(2,1)}, bf16[128,512]{1,0:T(8,128)(2,1)S(1)}, u32[]{:S(2)}, u32[]{:S(2)}) %collective-permute-start.1) | collective-permute-done | bytes 131104 | tf_op jit(solution)/shard_map/ppermute | solution.py:12
  12.7 0.0 collective-permute-start.2
  12.7 0.8 %copy.9.sources = s32[8,1,4]{2,1,0:T(1,128)S(1)} copy(s32[8,1,4]{0,2,1:T(4,128)} %param.10) | data formatting | bytes 256 | tf_op args[2]
  13.5 0.7 %copy.10.counts = s32[8,1]{1,0:T(8,128)S(1)} copy(s32[8,1]{0,1:T(1,128)} %param.11) | data formatting | bytes 64 | tf_op args[3]
  14.2 0.8 %copy.11.targets = s32[8,4,4]{2,1,0:T(4,128)S(1)} copy(s32[8,4,4]{0,2,1:T(4,128)} %param.13) | data formatting | bytes 1024 | tf_op args[5]
  15.0 0.0 collective-permute-done.3.refs_4_
  15.0 0.0 collective-permute-done.refs_1_
  15.0 0.0 collective-permute-done.5.refs_6_
  15.0 0.0 collective-permute-done.2.refs_3_
  15.0 0.0 copy-start
  15.0 2.2 %copy-done = bf16[8,4,4,128,128]{4,3,2,1,0:T(8,128)(2,1)S(1)} copy-done((bf16[8,4,4,128,128]{4,3,2,1,0:T(8,128)(2,1)S(1)}, bf16[8,4,4,128,128]{4,3,2,1,0:T(8,128)(2,1)}, u32[]{:S(2)}) %copy-start) | copy-done | bytes 4194328
  17.2 0.0 copy-start.1
  17.2 1.2 %copy-done.1 = bf16[8,1,4,128,128]{4,3,2,1,0:T(8,128)(2,1)S(1)} copy-done((bf16[8,1,4,128,128]{4,3,2,1,0:T(8,128)(2,1)S(1)}, bf16[8,1,4,128,128]{4,3,2,1,0:T(8,128)(2,1)}, u32[]{:S(2)}) %copy-start.1) | copy-done | bytes 1048600
  18.4 0.0 copy-start.2
  18.4 0.9 %copy-done.2 = bf16[128,512]{1,0:T(8,128)(2,1)S(1)} copy-done((bf16[128,512]{1,0:T(8,128)(2,1)S(1)}, bf16[128,512]{1,0:T(8,128)(2,1)}, u32[]{:S(2)}) %copy-start.2) | copy-done | bytes 131096
  19.3 3.8 %couple.1 = (bf16[128,512]{1,0:T(8,128)(2,1)S(1)}, bf16[128,512]{1,0:T(8,128)(2,1)S(1)}, bf16[128,512]{1,0:T(8,128)(2,1)S(1)}, bf16[128,512]{1,0:T(8,128)(2,1)S(1)}) custom-call(s32[8,1,4]{2,1,0:T(1,128)S(1)} %copy.9.sources, s32[8,1]{1,0:T(8,128)S(1)} %copy.10.counts, s32[8,4,4]{2,1,0:T(4,128)S(1)} %copy.11.targets, bf16[128,512]{1,0:T(8,128)(2,1)S(1)} %copy-done.2, ...), custom_call_target="tpu_custom_call" | custom-call | flops 1073741824 | bytes 5242880 | tf_op jit(solution)/shard_map/couple/pallas_call | solution.py:115
  23.2 1.6 %collective-permute-start.6 = (bf16[128,512]{1,0:T(8,128)(2,1)S(1)}, bf16[128,512]{1,0:T(8,128)(2,1)S(1)}, u32[]{:S(2)}, u32[]{:S(2)}) collective-permute-start(bf16[128,512]{1,0:T(8,128)(2,1)S(1)} %get-tuple-element.10), channel_id=1, source_target_pairs={{0,1},{1,0},{2,3},{3,2},{4,5},{5,4},{6,7},{7,6},{8,9},{9,8},{10,11... | collective-permute-start | bytes 393224 | tf_op jit(solution)/shard_map/ppermute | solution.py:12
  24.8 2.6 %collective-permute-start.7 = (bf16[128,512]{1,0:T(8,128)(2,1)S(1)}, bf16[128,512]{1,0:T(8,128)(2,1)S(1)}, u32[]{:S(2)}, u32[]{:S(2)}) collective-permute-start(bf16[128,512]{1,0:T(8,128)(2,1)S(1)} %get-tuple-element.11), channel_id=1, source_target_pairs={{0,2},{1,3},{2,0},{3,1},{4,6},{5,7},{6,4},{7,5},{8,10},{9,11},{10,... | collective-permute-start | bytes 393224 | tf_op jit(solution)/shard_map/ppermute | solution.py:12
  27.4 0.2 collective-permute-start.8
  27.6 3.8 %collective-permute-done.6 = bf16[128,512]{1,0:T(8,128)(2,1)S(1)} collective-permute-done((bf16[128,512]{1,0:T(8,128)(2,1)S(1)}, bf16[128,512]{1,0:T(8,128)(2,1)S(1)}, u32[]{:S(2)}, u32[]{:S(2)}) %collective-permute-start.6) | collective-permute-done | bytes 131104 | tf_op jit(solution)/shard_map/ppermute | solution.py:12
  31.4 6.3 %collective-permute-done.7 = bf16[128,512]{1,0:T(8,128)(2,1)S(1)} collective-permute-done((bf16[128,512]{1,0:T(8,128)(2,1)S(1)}, bf16[128,512]{1,0:T(8,128)(2,1)S(1)}, u32[]{:S(2)}, u32[]{:S(2)}) %collective-permute-start.7) | collective-permute-done | bytes 131104 | tf_op jit(solution)/shard_map/ppermute | solution.py:12
  37.8 0.0 collective-permute-done.8
  37.8 0.0 copy-done.3
  37.8 0.0 copy-done.4
  37.8 0.8 %multiply_add_fusion = f32[128,512]{1,0:T(8,128)} fusion(bf16[128,512]{1,0:T(8,128)(2,1)S(1)} %copy-done.2, bf16[128,512]{1,0:T(8,128)(2,1)S(1)} %collective-permute-done.8, bf16[128,512]{1,0:T(8,128)(2,1)S(1)} %collective-permute-done.7, bf16[128,512]{1,0:T(8,128)(2,1)S(1)} %collective-permute-done.6, bf16[128,512]{1,0:T(8,128)(2,1)S(1)} %get-tuple-element.9, ...), kind=kLoop, calls=%fused_computation | loop fusion | flops 720896 | bytes 920064 | tf_op jit(solution)/shard_map/add | solution.py:140
Async XLA Ops:
  0.0 37.8 %copy-start.3 = (f32[512]{0:T(512)S(1)}, f32[512]{0:T(512)}, u32[]{:S(2)}) copy-start(f32[512]{0:T(512)} %param.15) | copy-start | bytes 6148
  0.0 37.8 %copy-start.4 = (f32[128]{0:T(128)S(1)}, f32[128]{0:T(128)}, u32[]{:S(2)}) copy-start(f32[128]{0:T(128)} %param.14) | copy-start | bytes 1540
  0.0 8.7 %collective-permute-start.4 = (bf16[128,512]{1,0:T(8,128)(2,1)}, bf16[128,512]{1,0:T(8,128)(2,1)S(1)}, u32[]{:S(2)}, u32[]{:S(2)}) collective-permute-start(bf16[128,512]{1,0:T(8,128)(2,1)} %refs_0_.1), channel_id=1, source_target_pairs={{16,8},{20,12},{8,16},{12,20},{17,9},{21,13},{9,17},{13,21},{18,10... | collective-permute-start | bytes 393224 | tf_op jit(solution)/shard_map/ppermute | solution.py:12
  0.8 11.9 %collective-permute-start.1 = (bf16[128,512]{1,0:T(8,128)(2,1)}, bf16[128,512]{1,0:T(8,128)(2,1)S(1)}, u32[]{:S(2)}, u32[]{:S(2)}) collective-permute-start(bf16[128,512]{1,0:T(8,128)(2,1)} %refs_0_.1), channel_id=1, source_target_pairs={{8,0},{12,4},{0,8},{4,12},{24,16},{28,20},{16,24},{20,28},{9,1},{1... | collective-permute-start | bytes 393224 | tf_op jit(solution)/shard_map/ppermute | solution.py:12
  6.6 8.4 %collective-permute-start.3 = (bf16[128,512]{1,0:T(8,128)(2,1)}, bf16[128,512]{1,0:T(8,128)(2,1)S(1)}, u32[]{:S(2)}, u32[]{:S(2)}) collective-permute-start(bf16[128,512]{1,0:T(8,128)(2,1)} %refs_0_.1), channel_id=1, source_target_pairs={{16,4},{24,12},{4,16},{12,24},{17,5},{25,13},{5,17},{13,25},{18,6}... | collective-permute-start | bytes 393224 | tf_op jit(solution)/shard_map/ppermute | solution.py:12
  7.2 7.8 %collective-permute-start = (bf16[128,512]{1,0:T(8,128)(2,1)}, bf16[128,512]{1,0:T(8,128)(2,1)S(1)}, u32[]{:S(2)}, u32[]{:S(2)}) collective-permute-start(bf16[128,512]{1,0:T(8,128)(2,1)} %refs_0_.1), channel_id=1, source_target_pairs={{0,4},{4,0},{8,12},{12,8},{16,20},{20,16},{24,28},{28,24},{1,5},{5... | collective-permute-start | bytes 393224 | tf_op jit(solution)/shard_map/ppermute | solution.py:12
  8.7 6.3 %collective-permute-start.5 = (bf16[128,512]{1,0:T(8,128)(2,1)S(1)}, bf16[128,512]{1,0:T(8,128)(2,1)S(1)}, u32[]{:S(2)}, u32[]{:S(2)}) collective-permute-start(bf16[128,512]{1,0:T(8,128)(2,1)S(1)} %collective-permute-done.4.refs_5_), channel_id=1, source_target_pairs={{12,8},{8,12},{20,16},{16,20},{13,9},{9,13},{21,17},{17,21},{14,10... | collective-permute-start | bytes 393224 | tf_op jit(solution)/shard_map/ppermute | solution.py:12
  12.7 2.3 %collective-permute-start.2 = (bf16[128,512]{1,0:T(8,128)(2,1)S(1)}, bf16[128,512]{1,0:T(8,128)(2,1)S(1)}, u32[]{:S(2)}, u32[]{:S(2)}) collective-permute-start(bf16[128,512]{1,0:T(8,128)(2,1)S(1)} %collective-permute-done.1.refs_2_), channel_id=1, source_target_pairs={{4,0},{0,4},{12,8},{8,12},{20,16},{16,20},{28,24},{24,28},{5,1},{1... | collective-permute-start | bytes 393224 | tf_op jit(solution)/shard_map/ppermute | solution.py:12
  15.0 2.2 %copy-start = (bf16[8,4,4,128,128]{4,3,2,1,0:T(8,128)(2,1)S(1)}, bf16[8,4,4,128,128]{4,3,2,1,0:T(8,128)(2,1)}, u32[]{:S(2)}) copy-start(bf16[8,4,4,128,128]{4,3,2,1,0:T(8,128)(2,1)} %refs_8_.1) | copy-start | bytes 12582916
  17.2 1.2 %copy-start.1 = (bf16[8,1,4,128,128]{4,3,2,1,0:T(8,128)(2,1)S(1)}, bf16[8,1,4,128,128]{4,3,2,1,0:T(8,128)(2,1)}, u32[]{:S(2)}) copy-start(bf16[8,1,4,128,128]{4,3,2,1,0:T(8,128)(2,1)} %refs_7_.1) | copy-start | bytes 3145732
  18.4 0.9 %copy-start.2 = (bf16[128,512]{1,0:T(8,128)(2,1)S(1)}, bf16[128,512]{1,0:T(8,128)(2,1)}, u32[]{:S(2)}) copy-start(bf16[128,512]{1,0:T(8,128)(2,1)} %refs_0_.1) | copy-start | bytes 393220
  23.2 8.2 %collective-permute-start.6 = (bf16[128,512]{1,0:T(8,128)(2,1)S(1)}, bf16[128,512]{1,0:T(8,128)(2,1)S(1)}, u32[]{:S(2)}, u32[]{:S(2)}) collective-permute-start(bf16[128,512]{1,0:T(8,128)(2,1)S(1)} %get-tuple-element.10), channel_id=1, source_target_pairs={{0,1},{1,0},{2,3},{3,2},{4,5},{5,4},{6,7},{7,6},{8,9},{9,8},{10,11... | collective-permute-start | bytes 393224 | tf_op jit(solution)/shard_map/ppermute | solution.py:12
  24.8 12.9 %collective-permute-start.7 = (bf16[128,512]{1,0:T(8,128)(2,1)S(1)}, bf16[128,512]{1,0:T(8,128)(2,1)S(1)}, u32[]{:S(2)}, u32[]{:S(2)}) collective-permute-start(bf16[128,512]{1,0:T(8,128)(2,1)S(1)} %get-tuple-element.11), channel_id=1, source_target_pairs={{0,2},{1,3},{2,0},{3,1},{4,6},{5,7},{6,4},{7,5},{8,10},{9,11},{10,... | collective-permute-start | bytes 393224 | tf_op jit(solution)/shard_map/ppermute | solution.py:12
  27.4 10.3 %collective-permute-start.8 = (bf16[128,512]{1,0:T(8,128)(2,1)S(1)}, bf16[128,512]{1,0:T(8,128)(2,1)S(1)}, u32[]{:S(2)}, u32[]{:S(2)}) collective-permute-start(bf16[128,512]{1,0:T(8,128)(2,1)S(1)} %get-tuple-element.12), channel_id=1, source_target_pairs={{0,3},{1,2},{2,1},{3,0},{4,7},{5,6},{6,5},{7,4},{8,11},{9,10},{10,... | collective-permute-start | bytes 393224 | tf_op jit(solution)/shard_map/ppermute | solution.py:12
